TPU v7x, 32 devices: a whole 2x2x4 slice. The times are simulated.
32 devices in a mesh: seed: 2 (over core), dp: 4 (over y, x), tensor: 4 (over z).
Axes of the slice: x: 2, y: 2, z: 4, core: 2. Of those that a mesh axis runs over, the one named last changes fastest.
Arguments:
- hidden: bfloat16 [2, 64, 96, 2048], P('seed', 'dp', None, 'tensor'), may hold values from -24 to 24
- norm_gain: float32 [2, 2048], P('seed'), may hold values from 0.25 to 1.75
- lm_head: bfloat16 [2, 2048, 4096], P('seed', None, 'tensor'), may hold values from -3 to 3
- targets: int32 [64, 96], P('dp'), may hold values from 0 to 4095
- lengths: int32 [64], P('dp'), may hold values from 24 to 96
Outputs:
- token_scores: float32 [2, 64, 96], P('seed', 'dp')
- ensemble: float32 [64], P('dp')
- centered: float32 [64], P('dp')
All inputs are finite; a program needn't handle non-finite values.
Results may differ from a plain program's by a relative error of at most 0.0003.
The roundings to bfloat16 on the way count: a program that leaves them out, or rounds other values in their place, can miss the bound.
Values may be sent and summed in bfloat16 or wider, within the bound.
A program may use at most 128 MiB of HBM per device.

v0:
```python
import jax
import jax.numpy as jnp
from jax import lax
from jax.sharding import PartitionSpec as P

rms_epsilon = 1e-05


def shards(hidden, norm_gain, lm_head, targets, lengths):
    per_group, seq_len, own_width = (hidden.shape[1], hidden.shape[2], hidden.shape[3])
    full_width = norm_gain.shape[1]
    own_vocab = lm_head.shape[2]
    row_count = per_group * seq_len
    weight = lm_head[0]
    gain = norm_gain[0]
    whole = lax.all_gather(hidden, "tensor", axis=3, tiled=True)
    flat = whole.reshape(row_count, full_width).astype(jnp.float32)
    mean_sq = jnp.mean(flat * flat, axis=1, keepdims=True)
    normed = (flat * lax.rsqrt(mean_sq + rms_epsilon) * gain).astype(jnp.bfloat16)
    logits = jnp.dot(normed, weight, preferred_element_type=jnp.float32)
    first_column = lax.axis_index("tensor") * own_vocab
    column = jnp.arange(own_vocab, dtype=jnp.int32) + first_column
    onehot = column[None, :] == targets.reshape(row_count)[:, None]
    top_value = lax.pmax(jnp.max(logits, axis=1), "tensor")
    scaled_exp = jnp.exp(logits - top_value[:, None])
    exp_mass, exp_square, exp_target = lax.psum(
        (
            jnp.sum(scaled_exp, axis=1),
            jnp.sum(scaled_exp * scaled_exp, axis=1),
            jnp.sum(jnp.where(onehot, scaled_exp, 0.0), axis=1),
        ),
        "tensor",
    )
    spread = jnp.maximum(
        exp_square / (exp_mass * exp_mass) - 2.0 * exp_target / exp_mass + 1.0, 0.0
    )
    scores = jnp.sqrt(spread).reshape(per_group, seq_len)
    position = jnp.arange(seq_len, dtype=jnp.int32)
    valid = position[None, :] < lengths[:, None]
    token_scores = jnp.where(valid, scores, jnp.float32(0.0))
    example_scores = jnp.sum(token_scores, axis=1) / lengths.astype(jnp.float32)
    members = lax.axis_size("seed")
    groups = lax.axis_size("dp")
    ensemble = lax.psum(example_scores, "seed") / members
    batch_total = lax.psum(jnp.sum(ensemble), "dp")
    centered = ensemble - batch_total / (per_group * groups)
    return (token_scores[None, :, :], ensemble, centered)


def solution(mesh):
    return jax.shard_map(
        shards,
        mesh=mesh,
        in_specs=(
            P("seed", "dp", None, "tensor"),
            P("seed", None),
            P("seed", None, "tensor"),
            P("dp", None),
            P("dp"),
        ),
        out_specs=(P("seed", "dp", None), P("dp"), P("dp")),
        check_vma=False,
    )
```

profile of v0, /device:TPU:0, one launch (start us, length us, event | category | flops | bytes accessed | tf_op | source)
XLA Modules:
  0.0 197.2 jit_solution(9781393687701684352)
XLA Ops:
  7.2 0.0 copy-start.1
  7.2 0.0 all-gather.2.cloned.1.call-start
  7.2 0.7 all-gather.2.cloned.1.call-update
  7.9 0.8 eq.16
  8.7 119.0 %all-gather.2.cloned.1.call-done = bf16[1,16,96,2048]{3,2,1,0:T(8,128)(2,1)} async-done(((bf16[1,16,96,512]{3,2,1,0:T(8,128)(2,1)}), bf16[1,16,96,2048]{3,2,1,0:T(8,128)(2,1)}) %all-gather.2.cloned.1.call-update) | async-done | bytes 6291472 | tf_op jit(solution)/shard_map/all_gather | solution.py:16
  127.6 0.0 copy-start
  127.6 4.2 %fusion = f32[16,96]{1,0:T(8,128)S(1)} fusion(bf16[1,16,96,2048]{3,2,1,0:T(8,128)(2,1)} %all-gather.2.cloned.1.call-done), kind=kLoop, calls=%fused_computation.2 | loop fusion | flops 9435648 | bytes 6297600 | tf_op jit(solution)/shard_map/reduce_sum | solution.py:18
  131.9 0.0 copy-done.1
  131.9 0.3 copy-done
  132.2 1.5 fusion.2
  133.7 10.6 %fusion.8 = (f32[1536]{0:T(1024)S(1)}, f32[1536,1024]{0,1:T(8,128)}) fusion(bf16[1536,2048]{1,0:T(8,128)(2,1)S(1)} %bitcast.8, bf16[1,2048,1024]{2,1,0:T(8,128)(2,1)} %param.7), kind=kOutput, calls=%fused_computation.22 | convolution fusion | flops 6444022272 | bytes 16783360 | tf_op jit(solution)/shard_map/dot_general | solution.py:20
  144.3 8.9 %pmax.7 = f32[1536]{0:T(1024)S(1)} all-reduce(f32[1536]{0:T(1024)S(1)} %get-tuple-element.11), channel_id=1, replica_groups=mesh['seed'=2,'dp'=4,'tensor'=4] {'tensor'}, use_global_device_ids=true, to_apply=%region_2.0 | all-reduce | flops 1536 | bytes 12288 | tf_op jit(solution)/shard_map/pmax | solution.py:24
  153.2 4.1 %multiply_reduce_fusion = (f32[1536]{0:T(1024)S(1)}, f32[1536]{0:T(1024)S(1)}, f32[1536]{0:T(1024)S(1)}) fusion(f32[1536,1024]{0,1:T(8,128)} %get-tuple-element.12, f32[1536]{0:T(1024)S(1)} %pmax.7, s32[1536]{0:T(1024)S(1)} %eq.16, s32[1024]{0:T(1024)S(1)} %iota_add_fusion), kind=kLoop, calls=%fused_computation.6 | loop fusion | flops 11005440 | bytes 6326272 | tf_op jit(solution)/shard_map/reduce_sum | solution.py:29
  157.3 17.4 %all-reduce = (f32[1536]{0:T(1024)S(1)}, f32[1536]{0:T(1024)S(1)}, f32[1536]{0:T(1024)S(1)}) all-reduce(f32[1536]{0:T(1024)S(1)} %get-tuple-element.4, f32[1536]{0:T(1024)S(1)} %get-tuple-element.5, f32[1536]{0:T(1024)S(1)} %get-tuple-element.3), channel_id=1, replica_groups=mesh['seed'=2,'dp'=4,'tensor'=4] {'tensor'}, use_global_device_ids=true, to_apply=%region_6.7 | all-reduce | flops 4608 | bytes 36864 | tf_op jit(solution)/shard_map/psum | solution.py:26
  174.7 0.1 reshape.81
  174.8 0.1 reshape.80
  174.9 0.0 copy-done.2
  174.9 0.2 select_reduce_fusion.1
  175.1 2.5 %psum.38 = f32[16]{0:T(128)S(1)} all-reduce(f32[16]{0:T(128)S(1)} %convert_divide_fusion), channel_id=1, replica_groups=mesh['seed'=2,'dp'=4,'tensor'=4] {'seed'}, use_global_device_ids=true, to_apply=%region_10.11 | all-reduce | flops 16 | bytes 128 | tf_op jit(solution)/shard_map/psum | solution.py:44
  177.5 0.6 fusion.7
  178.1 10.4 %psum.39 = f32[]{:T(128)} all-reduce(f32[]{:T(128)} %get-tuple-element.9), channel_id=1, replica_groups=mesh['seed'=2,'dp'=4,'tensor'=4] {'dp'}, use_global_device_ids=true, to_apply=%region_12.13 | all-reduce | flops 1 | bytes 8 | tf_op jit(solution)/shard_map/psum | solution.py:45
  188.5 0.7 fusion.6
  189.9 0.5 broadcast_subtract_fusion
  190.4 0.0 copy-done.3
  (6 shorter events, 0.0 us)
Async XLA Ops:
  7.2 124.7 %copy-start.1 = (f32[1,2048]{1,0:T(1,128)S(1)}, f32[1,2048]{1,0:T(1,128)}, u32[]{:S(2)}) copy-start(f32[1,2048]{1,0:T(1,128)} %param.6) | copy-start | bytes 24580
  7.2 120.5 %all-gather.2.cloned.1.call-start = ((), (), s32[]{:S(2)}) async-start(), calls=%async_computation | async-start | bytes 7864320 | tf_op jit(solution)/shard_map/all_gather | solution.py:16
  127.6 4.6 %copy-start = (bf16[1,16,96,2048]{3,2,1,0:T(8,128)(2,1)S(1)}, bf16[1,16,96,2048]{3,2,1,0:T(8,128)(2,1)}, u32[]{:S(2)}) copy-start(bf16[1,16,96,2048]{3,2,1,0:T(8,128)(2,1)} %all-gather.2.cloned.1.call-done) | copy-start | bytes 18874372
  144.3 30.5 %copy-start.2 = (s32[16]{0:T(128)S(1)}, s32[16]{0:T(128)}, u32[]{:S(2)}) copy-start(s32[16]{0:T(128)} %param.9) | copy-start | bytes 196
  178.1 12.2 %copy-start.3 = (f32[16]{0:T(128)}, f32[16]{0:T(128)S(1)}, u32[]{:S(2)}) copy-start(f32[16]{0:T(128)S(1)} %get-tuple-element.10) | copy-start | bytes 196
Sparse Core Ops, SparseCore 0:
  9.6 118.0 all-gather.1
where the time goes:
time: 198 us; the launch traced here: 197 us
  waiting for transfers between devices  120 us (61%)
  blocking collectives  39.2 us (20%)
  between operations  14.7 us (7%)
  other arithmetic  11.8 us (6%)
  matrix products  10.6 us (5%)
    all_gather x1, waiting for transfers between devices, shards(): whole = lax.all_gather(hidden, 'tensor', axis=3, tiled=True)  119 us
    psum x1, blocking collectives, shards(): lax.psum((jnp.sum(scaled_exp, axis=1), jnp.sum(scaled_exp * scaled_exp, a...  17.4 us
    dot_general x1, matrix products, shards(): logits = jnp.dot(normed, weight, preferred_element_type=jnp.float32)  10.6 us
    psum x1, blocking collectives, shards(): batch_total = lax.psum(jnp.sum(ensemble), 'dp')  10.4 us
    pmax x1, blocking collectives, shards(): top_value = lax.pmax(jnp.max(logits, axis=1), 'tensor')  8.91 us
    reduce_sum x1, other arithmetic, shards(): mean_sq = jnp.mean(flat * flat, axis=1, keepdims=True)  4.24 us
    reduce_sum x1, other arithmetic, shards(): jnp.sum(scaled_exp * scaled_exp, axis=1)  4.07 us
  transfers between devices with their start and end apart: 1, of which 1 were waited for; matrix products, arithmetic and copies ran while one was open for 0% of the time, Pallas kernels for 0%

commit v1 on v0

v1 whole, which is shorter than its diff:
```python
import functools

import jax
import jax.numpy as jnp
from jax import lax
from jax.experimental import pallas as pl
from jax.experimental.pallas import tpu as pltpu
from jax.sharding import PartitionSpec as P

rms_epsilon = 1e-05
MESH = pl.DeviceIdType.MESH


def line_kernel(
    n, chunk, x_ref, gain_ref, w_ref, tgt_ref, out_ref,
    buf, w_buf, stats, own_sem, w_sem, send_sem, recv_sem, stat_send, stat_recv,
):
    me = lax.axis_index("tensor")
    rows, own = x_ref.shape
    vocab = w_ref.shape[1]
    chunks = rows // chunk
    right = jnp.minimum(me + 1, n - 1)
    left = jnp.maximum(me - 1, 0)

    barrier = pltpu.get_barrier_semaphore()
    for k in range(1, n):
        pl.semaphore_signal(
            barrier, inc=1, device_id={"tensor": lax.rem(me + k, n)}, device_id_type=MESH
        )
    pl.semaphore_wait(barrier, n - 1)

    def span(c):
        return pl.ds(pl.multiple_of(c * chunk, chunk), chunk)

    def hop(src, block, c, way):
        return pltpu.make_async_remote_copy(
            src_ref=src,
            dst_ref=buf.at[block, span(c)],
            send_sem=send_sem.at[way, block, c],
            recv_sem=recv_sem.at[block, c],
            device_id={"tensor": right if way == 0 else left},
            device_id_type=MESH,
        )

    def first(c, carry):
        @pl.when(me < n - 1)
        def _():
            hop(x_ref.at[span(c)], me, c, 0).start()

        @pl.when(me > 0)
        def _():
            hop(x_ref.at[span(c)], me, c, 1).start()

        return carry

    lax.fori_loop(0, chunks, first, 0)
    own_copy = pltpu.make_async_copy(x_ref, buf.at[me], own_sem)
    own_copy.start()
    w_copy = pltpu.make_async_copy(w_ref, w_buf, w_sem)
    w_copy.start()

    def relay(d, c):
        @pl.when(me - d >= 0)
        def _():
            block = jnp.maximum(me - d, 0)
            copy = hop(buf.at[block, span(c)], block, c, 0)
            copy.wait_recv()

            @pl.when(me < n - 1)
            def _():
                copy.start()

        @pl.when(me + d < n)
        def _():
            block = jnp.minimum(me + d, n - 1)
            copy = hop(buf.at[block, span(c)], block, c, 1)
            copy.wait_recv()

            @pl.when(me > 0)
            def _():
                copy.start()

    def middle(i, carry):
        relay(1 + i // chunks, lax.rem(i, chunks))
        return carry

    lax.fori_loop(0, (n - 2) * chunks, middle, 0)
    own_copy.wait()
    w_copy.wait()

    def stat_copy(k, c):
        return pltpu.make_async_remote_copy(
            src_ref=stats.at[me, c],
            dst_ref=stats.at[me, c],
            send_sem=stat_send.at[k, c],
            recv_sem=stat_recv.at[me, c],
            device_id={"tensor": lax.rem(me + k, n)},
            device_id_type=MESH,
        )

    def last(c, carry):
        relay(n - 1, c)
        at = span(c)
        square = jnp.zeros((chunk, 1), jnp.float32)
        for j in range(n):
            part = buf[j, at].astype(jnp.float32)
            square += jnp.sum(part * part, axis=1, keepdims=True)
        scale = lax.rsqrt(square / (own * n) + rms_epsilon)
        logits = jnp.zeros((chunk, vocab), jnp.float32)
        for j in range(n):
            part = buf[j, at].astype(jnp.float32)
            normed = (part * scale * gain_ref[j]).astype(jnp.bfloat16)
            logits += jnp.dot(
                normed, w_buf[pl.ds(j * own, own), :], preferred_element_type=jnp.float32
            )
        top = jnp.max(logits, axis=1, keepdims=True)
        mass = jnp.exp(logits - top)
        column = lax.broadcasted_iota(jnp.int32, (chunk, vocab), 1) + me * vocab
        hit = jnp.where(column == tgt_ref[at, :], mass, 0.0)
        lane = lax.broadcasted_iota(jnp.int32, (chunk, 128), 1)
        packed = jnp.where(
            lane == 0,
            top,
            jnp.where(
                lane == 1,
                jnp.sum(mass, axis=1, keepdims=True),
                jnp.where(
                    lane == 2,
                    jnp.sum(mass * mass, axis=1, keepdims=True),
                    jnp.sum(hit, axis=1, keepdims=True),
                ),
            ),
        )
        stats[me, c] = packed.T[:8]
        for k in range(1, n):
            stat_copy(k, c).start()
        return carry

    lax.fori_loop(0, chunks, last, 0)

    def finish(c, carry):
        for k in range(1, n):
            peer = lax.rem(me + k, n)
            pltpu.make_async_remote_copy(
                src_ref=stats.at[peer, c],
                dst_ref=stats.at[peer, c],
                send_sem=stat_send.at[k, c],
                recv_sem=stat_recv.at[peer, c],
                device_id={"tensor": peer},
                device_id_type=MESH,
            ).wait_recv()
        top = stats[0, c, 0:1]
        for j in range(1, n):
            top = jnp.maximum(top, stats[j, c, 0:1])
        mass = jnp.zeros_like(top)
        square = jnp.zeros_like(top)
        hit = jnp.zeros_like(top)
        for j in range(n):
            factor = jnp.exp(stats[j, c, 0:1] - top)
            mass += stats[j, c, 1:2] * factor
            square += stats[j, c, 2:3] * (factor * factor)
            hit += stats[j, c, 3:4] * factor
        spread = square / (mass * mass) - 2.0 * hit / mass + 1.0
        out_ref[pl.ds(c, 1), :] = jnp.sqrt(jnp.maximum(spread, 0.0))
        return carry

    lax.fori_loop(0, chunks, finish, 0)

    def drain(i, carry):
        block, c = i // chunks, lax.rem(i, chunks)

        @pl.when((me < n - 1) & (block <= me))
        def _():
            hop(buf.at[block, span(c)], block, c, 0).wait_send()

        @pl.when((me > 0) & (block >= me))
        def _():
            hop(buf.at[block, span(c)], block, c, 1).wait_send()

        return carry

    lax.fori_loop(0, n * chunks, drain, 0)

    def drain_stats(c, carry):
        for k in range(1, n):
            stat_copy(k, c).wait_send()
        return carry

    lax.fori_loop(0, chunks, drain_stats, 0)


def row_errors(x, gain, weight, wanted, n):
    rows, own = x.shape
    depth, vocab = weight.shape
    chunk = rows
    while chunk % 256 == 0 and n * (rows // chunk) < 128 and chunk > 128:
        chunk //= 2
    if rows % 128 == 0 and n * (rows // 128) <= 128:
        chunk = 128
    chunks = rows // chunk
    dma = pltpu.SemaphoreType.DMA
    out = pl.pallas_call(
        functools.partial(line_kernel, n, chunk),
        out_shape=jax.ShapeDtypeStruct((chunks, chunk), jnp.float32),
        in_specs=[
            pl.BlockSpec(memory_space=pl.ANY),
            pl.BlockSpec(memory_space=pltpu.VMEM),
            pl.BlockSpec(memory_space=pl.ANY),
            pl.BlockSpec(memory_space=pltpu.VMEM),
        ],
        out_specs=pl.BlockSpec(memory_space=pltpu.VMEM),
        scratch_shapes=[
            pltpu.VMEM((n, rows, own), x.dtype),
            pltpu.VMEM((depth, vocab), weight.dtype),
            pltpu.VMEM((n, chunks, 8, chunk), jnp.float32),
            dma,
            dma,
            dma((2, n, chunks)),
            dma((n, chunks)),
            dma((n, chunks)),
            dma((n, chunks)),
        ],
        compiler_params=pltpu.CompilerParams(
            collective_id=0, has_side_effects=True, vmem_limit_bytes=60 * 1024 * 1024
        ),
        name="line_scores",
    )(x, gain.reshape(n, 1, own), weight, wanted.reshape(rows, 1))
    return out.reshape(rows)


def shards(hidden, norm_gain, lm_head, targets, lengths):
    per_group, seq_len, own_width = (hidden.shape[1], hidden.shape[2], hidden.shape[3])
    row_count = per_group * seq_len
    flat = hidden.reshape(row_count, own_width)
    scores = row_errors(
        flat, norm_gain[0], lm_head[0], targets, lax.axis_size("tensor")
    ).reshape(per_group, seq_len)
    position = jnp.arange(seq_len, dtype=jnp.int32)
    valid = position[None, :] < lengths[:, None]
    token_scores = jnp.where(valid, scores, jnp.float32(0.0))
    example_scores = jnp.sum(token_scores, axis=1) / lengths.astype(jnp.float32)
    members = lax.axis_size("seed")
    groups = lax.axis_size("dp")
    ensemble = lax.psum(example_scores, "seed") / members
    batch_total = lax.psum(jnp.sum(ensemble), "dp")
    centered = ensemble - batch_total / (per_group * groups)
    return (token_scores[None, :, :], ensemble, centered)


def solution(mesh):
    return jax.shard_map(
        shards,
        mesh=mesh,
        in_specs=(
            P("seed", "dp", None, "tensor"),
            P("seed", None),
            P("seed", None, "tensor"),
            P("dp", None),
            P("dp"),
        ),
        out_specs=(P("seed", "dp", None), P("dp"), P("dp")),
        check_vma=False,
    )
```

time: 198 us -> 140 us (0.71)
  waiting for transfers between devices: 120 us -> 0 us
  Pallas kernels: 0 us -> 119 us
  blocking collectives: 39.2 us -> 13 us
  between operations: 14.7 us -> 1.3 us
  matrix products: 10.6 us -> 0 us
  other arithmetic: 11.8 us -> 1.97 us
  local copies, waits for them, and re-layouts: 1.26 us -> 3.8 us
    pallas_call x0 -> x1, Pallas kernels: none -> 119 us  [row_errors(): pl.pallas_call(functools.partial(line_kernel, n, chunk), out_shape=jax.Sh...]
    all_gather x1 -> x0, waiting for transfers between devices: 119 us -> none  [shards(): whole = lax.all_gather(hidden, 'tensor', axis=3, tiled=True)]
    psum x1 -> x0, blocking collectives: 17.4 us -> none  [shards(): lax.psum((jnp.sum(scaled_exp, axis=1), jnp.sum(scaled_exp * scaled_exp, a...]
    dot_general x1 -> x0, matrix products: 10.6 us -> none  [shards(): logits = jnp.dot(normed, weight, preferred_element_type=jnp.float32)]
    pmax x1 -> x0, blocking collectives: 8.91 us -> none  [shards(): top_value = lax.pmax(jnp.max(logits, axis=1), 'tensor')]
    reduce_sum x2 -> x0, other arithmetic: 8.31 us -> none  [the longest x1 4.24 us: shards(): mean_sq = jnp.mean(flat * flat, axis=1, keepdims=True)]
    reshape x2 -> x1, local copies, waits for them, and re-layouts: 0.14 us -> 2.25 us  [row_errors(): wanted.reshape(rows, 1)]
  transfers between devices with their start and end apart: 1 -> 0, of which waited for: 1 -> 0; matrix products, arithmetic and copies ran while one was open for 0% -> 0% of each run, Pallas kernels for 0% -> 0%
where the time goes in v1:
time: 140 us; the launch traced here: 139 us
  Pallas kernels  119 us (85%)
  blocking collectives  13 us (9%)
  local copies, waits for them, and re-layouts  3.8 us (3%)
  other arithmetic  1.97 us (1%)
    pallas_call x1, Pallas kernels, row_errors(): pl.pallas_call(functools.partial(line_kernel, n, chunk), out_shape=jax.Sh...  119 us
    psum x1, blocking collectives, shards(): batch_total = lax.psum(jnp.sum(ensemble), 'dp')  10.5 us

profile of v1, /device:TPU:0, one launch (start us, length us, event | category | flops | bytes accessed | tf_op | source)
XLA Modules:
  0.0 139.0 jit_solution(13583684096830890918)
XLA Ops:
  0.6 0.0 copy-start
  0.6 2.3 %reshape.52.tgt_ref = s32[1536,1]{1,0:T(8,128)} reshape(s32[16,96]{1,0:T(8,128)} %param.8) | data formatting | bytes 12288 | tf_op jit(solution)/shard_map/reshape | solution.py:227
  2.9 119.0 %line_scores.1 = f32[12,128]{1,0:T(8,128)} custom-call(bf16[1536,512]{1,0:T(8,128)(2,1)} %bitcast.4, f32[4,1,512]{2,1,0:T(1,128)} %bitcast.5, bf16[2048,1024]{1,0:T(8,128)(2,1)} %bitcast.3, s32[1536,1]{1,0:T(8,128)} %reshape.52.tgt_ref), custom_call_target="tpu_custom_call" | custom-call | tf_op jit(solution)/shard_map/line_scores/pallas_call | solution.py:202
  121.9 0.8 reshape_reshape.6
  122.7 0.0 copy-done
  122.7 0.2 select_reduce_fusion
  122.8 2.5 %psum.14 = f32[16]{0:T(128)S(1)} all-reduce(f32[16]{0:T(128)S(1)} %convert_divide_fusion), channel_id=1, replica_groups=mesh['seed'=2,'dp'=4,'tensor'=4] {'seed'}, use_global_device_ids=true, to_apply=%region_1.2 | all-reduce | flops 16 | bytes 128 | tf_op jit(solution)/shard_map/psum | solution.py:244
  125.3 0.8 reshape_reshape.5
  126.1 0.7 fusion
  126.8 0.6 fusion.1
  127.4 0.0 copy-start.1
  127.4 10.5 %psum.15 = f32[]{:T(128)} all-reduce(f32[]{:T(128)} %get-tuple-element.3), channel_id=1, replica_groups=mesh['seed'=2,'dp'=4,'tensor'=4] {'dp'}, use_global_device_ids=true, to_apply=%region_3.4 | all-reduce | flops 1 | bytes 8 | tf_op jit(solution)/shard_map/psum | solution.py:245
  138.5 0.5 broadcast_subtract_fusion
  139.0 0.0 copy-done.1
  (1 shorter events, 0.0 us)
Async XLA Ops:
  0.6 122.0 %copy-start = (s32[16]{0:T(128)S(1)}, s32[16]{0:T(128)}, u32[]{:S(2)}) copy-start(s32[16]{0:T(128)} %param.9) | copy-start | bytes 196
  127.4 11.7 %copy-start.1 = (f32[16]{0:T(128)}, f32[16]{0:T(128)S(1)}, u32[]{:S(2)}) copy-start(f32[16]{0:T(128)S(1)} %get-tuple-element.4) | copy-start | bytes 196

commit v2 on v1

--- a/solution.py
+++ b/solution.py
@@ -228,6 +228,70 @@
     return out.reshape(rows)
 
 
+def totals_kernel(members, groups, per_group, mine_ref, out_ref, parts, send_sem, recv_sem):
+    seed, group = lax.axis_index("seed"), lax.axis_index("dp")
+    count = members * groups
+    me = seed * groups + group
+
+    def device(peer):
+        return {"seed": peer // groups, "dp": lax.rem(peer, groups)}
+
+    barrier = pltpu.get_barrier_semaphore()
+    for k in range(1, count):
+        pl.semaphore_signal(
+            barrier, inc=1, device_id=device(lax.rem(me + k, count)), device_id_type=MESH
+        )
+    pl.semaphore_wait(barrier, count - 1)
+
+    def part(k, slot):
+        return pltpu.make_async_remote_copy(
+            src_ref=mine_ref,
+            dst_ref=parts.at[slot],
+            send_sem=send_sem.at[k],
+            recv_sem=recv_sem.at[slot],
+            device_id=device(lax.rem(me + k, count)),
+            device_id_type=MESH,
+        )
+
+    for k in range(1, count):
+        part(k, me).start()
+    for k in range(1, count):
+        part(k, lax.rem(me + k, count)).wait_recv()
+    whole = mine_ref[...]
+    for k in range(1, count):
+        whole += parts[lax.rem(me + k, count)]
+    ensemble = mine_ref[...]
+    for k in range(1, members):
+        ensemble += parts[lax.rem(seed + k, members) * groups + group]
+    ensemble = ensemble / members
+    total = jnp.sum(whole, keepdims=True) / members
+    out_ref[0] = ensemble
+    out_ref[1] = ensemble - total / (per_group * groups)
+    for k in range(1, count):
+        part(k, me).wait_send()
+
+
+def group_totals(example_scores, members, groups):
+    per_group = example_scores.shape[0]
+    count = members * groups
+    width = -(-per_group // 128) * 128
+    padded = jnp.pad(example_scores[None, :], ((0, 7), (0, width - per_group)))
+    out = pl.pallas_call(
+        functools.partial(totals_kernel, members, groups, per_group),
+        out_shape=jax.ShapeDtypeStruct((2, 8, width), jnp.float32),
+        in_specs=[pl.BlockSpec(memory_space=pltpu.VMEM)],
+        out_specs=pl.BlockSpec(memory_space=pltpu.VMEM),
+        scratch_shapes=[
+            pltpu.VMEM((count, 8, width), jnp.float32),
+            pltpu.SemaphoreType.DMA((count,)),
+            pltpu.SemaphoreType.DMA((count,)),
+        ],
+        compiler_params=pltpu.CompilerParams(collective_id=1, has_side_effects=True),
+        name="group_totals",
+    )(padded)
+    return out[0, 0, :per_group], out[1, 0, :per_group]
+
+
 def shards(hidden, norm_gain, lm_head, targets, lengths):
     per_group, seq_len, own_width = (hidden.shape[1], hidden.shape[2], hidden.shape[3])
     row_count = per_group * seq_len
@@ -239,11 +303,9 @@
     valid = position[None, :] < lengths[:, None]
     token_scores = jnp.where(valid, scores, jnp.float32(0.0))
     example_scores = jnp.sum(token_scores, axis=1) / lengths.astype(jnp.float32)
-    members = lax.axis_size("seed")
-    groups = lax.axis_size("dp")
-    ensemble = lax.psum(example_scores, "seed") / members
-    batch_total = lax.psum(jnp.sum(ensemble), "dp")
-    centered = ensemble - batch_total / (per_group * groups)
+    ensemble, centered = group_totals(
+        example_scores, lax.axis_size("seed"), lax.axis_size("dp")
+    )
     return (token_scores[None, :, :], ensemble, centered)
 
 

time: 140 us -> 133 us (0.950)
  blocking collectives: 13 us -> 0 us
  Pallas kernels: 119 us -> 125 us
  local copies, waits for them, and re-layouts: 3.8 us -> 5.6 us
    psum x2 -> x0, blocking collectives: 13 us -> none  [the longest x1 10.5 us: shards(): batch_total = lax.psum(jnp.sum(ensemble), 'dp')]
    pallas_call x0 -> x1, Pallas kernels: none -> 6.28 us  [group_totals(): pl.pallas_call(functools.partial(totals_kernel, members, groups, per_grou...]
where the time goes in v2:
time: 133 us; the launch traced here: 132 us
  Pallas kernels  125 us (94%)
  local copies, waits for them, and re-layouts  5.6 us (4%)
    pallas_call x1, Pallas kernels, row_errors(): pl.pallas_call(functools.partial(line_kernel, n, chunk), out_shape=jax.Sh...  119 us
    pallas_call x1, Pallas kernels, group_totals(): pl.pallas_call(functools.partial(totals_kernel, members, groups, per_grou...  6.28 us

profile of v2, /device:TPU:0, one launch (start us, length us, event | category | flops | bytes accessed | tf_op | source)
XLA Modules:
  0.0 132.4 jit_solution(10798848966561308777)
XLA Ops:
  0.6 0.0 copy-start
  0.6 2.3 %reshape.52.tgt_ref = s32[1536,1]{1,0:T(8,128)} reshape(s32[16,96]{1,0:T(8,128)} %param.8) | data formatting | bytes 12288 | tf_op jit(solution)/shard_map/reshape | solution.py:227
  2.9 119.0 %line_scores.1 = f32[12,128]{1,0:T(8,128)} custom-call(bf16[1536,512]{1,0:T(8,128)(2,1)} %bitcast.10, f32[4,1,512]{2,1,0:T(1,128)} %bitcast.11, bf16[2048,1024]{1,0:T(8,128)(2,1)} %bitcast.9, s32[1536,1]{1,0:T(8,128)} %reshape.52.tgt_ref), custom_call_target="tpu_custom_call" | custom-call | tf_op jit(solution)/shard_map/line_scores/pallas_call | solution.py:202
  121.9 0.8 reshape_reshape.6
  122.7 0.0 copy-done
  122.7 0.2 select_reduce_fusion
  122.8 0.8 reshape_reshape.5
  123.6 0.7 fusion
  124.3 0.6 pad.4.mine_ref
  124.9 6.3 %group_totals.1 = f32[2,8,128]{2,1,0:T(8,128)} custom-call(f32[8,128]{1,0:T(8,128)} %pad.4.mine_ref), custom_call_target="tpu_custom_call" | custom-call | tf_op jit(solution)/shard_map/group_totals/pallas_call | solution.py:279
  131.2 1.2 slice_bitcast_fusion
  (1 shorter events, 0.0 us)
Async XLA Ops:
  0.6 122.0 %copy-start = (s32[16]{0:T(128)S(1)}, s32[16]{0:T(128)}, u32[]{:S(2)}) copy-start(s32[16]{0:T(128)} %param.9) | copy-start | bytes 196
